TPU v7x, 32 devices: a whole 2x2x4 slice. The times are simulated.
32 devices in a mesh: groups: 2 (over y), seq: 4 (over z), batch: 2 (over x), head: 2 (over core).
Axes of the slice: x: 2, y: 2, z: 4, core: 2. Of those that a mesh axis runs over, the one named last changes fastest.
Arguments:
- queries: bfloat16 [64, 64, 128], P(('groups', 'seq', 'batch'), 'head'), parts along dimension 0, may hold values from -16 to 16
- fresh_token_keys: bfloat16 [64, 8, 128], P(('groups', 'seq', 'batch'), 'head'), parts along dimension 0, may hold values from -12 to 12
- fresh_token_values: bfloat16 [64, 8, 128], P(('groups', 'seq', 'batch'), 'head'), parts along dimension 0, may hold values from -6 to 6
- shared_prefix_keys: bfloat16 [16384, 8, 128], P(('groups', 'seq'), 'head'), parts along dimension 0, may hold values from -6 to 6
- shared_prefix_values: bfloat16 [16384, 8, 128], P(('groups', 'seq'), 'head'), parts along dimension 0, may hold values from -6 to 6
- sequence_suffix_keys: bfloat16 [64, 192, 8, 128], P(('groups', 'seq', 'batch'), None, 'head'), parts along dimension 0, may hold values from -8 to 8
- sequence_suffix_values: bfloat16 [64, 192, 8, 128], P(('groups', 'seq', 'batch'), None, 'head'), parts along dimension 0, may hold values from -6 to 6
- suffix_lengths: int32 [64], P(('groups', 'seq', 'batch')), parts along dimension 0, may hold values from 0 to 192, as said below
Outputs:
- context: bfloat16 [64, 64, 128], P(('groups', 'seq', 'batch'), 'head'), parts along dimension 0
There are 2 independent parts, one for each index of `groups`. A program takes and returns all parts, laid end to end along the dimension named above; each array names one. Nothing has to cross between parts.
Inputs may be any that keep to these rules, and one draw needn't show every extreme that they name: `suffix_lengths`: slots at and beyond a sequence's length hold no token. Some sequence has all 192 slots live in every draw.
All inputs are finite; a program needn't handle non-finite values.
Results may differ from a plain program's by a relative error of at most 0.002.
Values may be sent and summed in bfloat16 or wider, within the bound.
A program may use at most 64 MiB of HBM per device.

v0:
```python
import math

import jax
import jax.numpy as jnp
from jax import lax
from jax.sharding import PartitionSpec as P


def prefix_block(query_rows, block_keys, block_values, inv_root):
    scores = (
        lax.dot_general(
            query_rows, block_keys, (((1,), (1,)), ((), ())), preferred_element_type=jnp.float32
        )
        * inv_root
    )
    maxima = jnp.max(scores, axis=1)
    weights = jnp.exp(scores - maxima[:, None]).astype(jnp.bfloat16)
    totals = jnp.sum(weights, axis=1, dtype=jnp.float32)
    outputs = jnp.dot(weights, block_values, preferred_element_type=jnp.float32)
    return (maxima, totals, outputs)


def body(
    queries,
    fresh_token_keys,
    fresh_token_values,
    shared_prefix_keys,
    shared_prefix_values,
    sequence_suffix_keys,
    sequence_suffix_values,
    suffix_lengths,
):
    own_count, head_count, width = queries.shape
    kv_count = shared_prefix_keys.shape[1]
    query_group = head_count // kv_count
    inv_root = 1.0 / math.sqrt(width)
    seq_count = lax.axis_size("seq")
    gathered = lax.all_gather(queries, "seq", axis=0, tiled=True)
    row_count = gathered.shape[0]
    grouped = gathered.reshape(row_count, kv_count, query_group, width)
    maxima_list = []
    totals_list = []
    outputs_list = []
    for kv_head in range(kv_count):
        query_rows = grouped[:, kv_head].reshape(row_count * query_group, width)
        maxima, totals, outputs = prefix_block(
            query_rows, shared_prefix_keys[:, kv_head], shared_prefix_values[:, kv_head], inv_root
        )
        maxima_list.append(maxima.reshape(row_count, query_group))
        totals_list.append(totals.reshape(row_count, query_group))
        outputs_list.append(outputs.reshape(row_count, query_group, width))
    block_max = jnp.stack(maxima_list, axis=1).reshape(row_count, head_count)
    block_total = jnp.stack(totals_list, axis=1).reshape(row_count, head_count)
    block_out = jnp.stack(outputs_list, axis=1).reshape(row_count, head_count, width)
    own_rows = queries.reshape(own_count, kv_count, query_group, width)
    own_scores = (
        jnp.einsum("bgqd,bgd->bgq", own_rows, fresh_token_keys, preferred_element_type=jnp.float32)
        * inv_root
    )
    recent = (
        jnp.einsum(
            "bgqd,bsgd->bgqs", own_rows, sequence_suffix_keys, preferred_element_type=jnp.float32
        )
        * inv_root
    )
    slot_count = sequence_suffix_keys.shape[1]
    live = (jnp.arange(slot_count, dtype=jnp.int32)[None, :] < suffix_lengths[:, None])[
        :, None, None, :
    ]
    local_max = jnp.maximum(
        own_scores, jnp.max(jnp.where(live, recent, own_scores[..., None]), axis=-1)
    )
    recent_weights = jnp.where(
        live, jnp.exp(jnp.where(live, recent - local_max[..., None], 0.0)), 0.0
    ).astype(jnp.bfloat16)
    own_weights = jnp.exp(own_scores - local_max).astype(jnp.bfloat16)
    local_total = jnp.sum(recent_weights, axis=-1, dtype=jnp.float32) + own_weights.astype(
        jnp.float32
    )
    local_out = jnp.einsum(
        "bgqs,bsgd->bgqd",
        recent_weights,
        sequence_suffix_values,
        preferred_element_type=jnp.float32,
    )
    local_out = (
        local_out
        + own_weights.astype(jnp.float32)[..., None]
        * fresh_token_values.astype(jnp.float32)[:, :, None, :]
    )
    local_max = local_max.reshape(own_count, head_count)
    local_total = local_total.reshape(own_count, head_count)
    local_out = local_out.reshape(own_count, head_count, width)
    state_shape = (seq_count, own_count, head_count)
    got_out, got_max, got_total = (
        lax.all_to_all(
            block_out.reshape(seq_count, own_count, head_count, width),
            "seq",
            split_axis=0,
            concat_axis=0,
            tiled=True,
        ),
        lax.all_to_all(
            block_max.reshape(state_shape), "seq", split_axis=0, concat_axis=0, tiled=True
        ),
        lax.all_to_all(
            block_total.reshape(state_shape), "seq", split_axis=0, concat_axis=0, tiled=True
        ),
    )
    highest = jnp.maximum(local_max, jnp.max(got_max, axis=0))
    block_scale = jnp.exp(got_max - highest[None])
    local_scale = jnp.exp(local_max - highest)
    total = local_total * local_scale + jnp.sum(got_total * block_scale, axis=0)
    numerator = local_out * local_scale[..., None] + jnp.sum(
        got_out * block_scale[..., None], axis=0
    )
    return (numerator / total[..., None]).astype(jnp.bfloat16)


def solution(mesh):
    in_specs = (
        P(("groups", "seq", "batch"), "head", None),
        P(("groups", "seq", "batch"), "head", None),
        P(("groups", "seq", "batch"), "head", None),
        P(("groups", "seq"), "head", None),
        P(("groups", "seq"), "head", None),
        P(("groups", "seq", "batch"), None, "head", None),
        P(("groups", "seq", "batch"), None, "head", None),
        P(("groups", "seq", "batch")),
    )
    out_specs = P(("groups", "seq", "batch"), "head", None)
    return jax.shard_map(body, mesh=mesh, in_specs=in_specs, out_specs=out_specs, check_vma=False)
```

profile of v0, /device:TPU:0, one launch (start us, length us, event | category | flops | bytes accessed | tf_op | source)
XLA Modules:
  0.0 72.7 jit_solution(282723957632736956)
XLA Ops:
  0.0 8.9 %fusion.19 = (bf16[2048,1,128]{2,1,0:T(2,128)(2,1)S(1)}, bf16[2048,1,128]{2,1,0:T(2,128)(2,1)}, bf16[2048,1,128]{2,1,0:T(2,128)(2,1)}, bf16[2048,1,128]{2,1,0:T(2,128)(2,1)}) fusion(bf16[2048,4,128]{2,1,0:T(4,128)(2,1)} %param.11), kind=kLoop, calls=%fused_computation.62 | loop fusion | bytes 4194304 | tf_op jit(solution)/shard_map/slice | solution.py:47
  8.9 15.1 %all_gather.3 = bf16[16,32,128]{2,1,0:T(8,128)(2,1)S(1)} all-gather(bf16[4,32,128]{2,1,0:T(8,128)(2,1)S(1)} %copy-done.5), channel_id=1, replica_groups=mesh['groups'=2,'seq'=4,'batch'=2,'head'=2] {'seq'}, dimensions={0}, use_global_device_ids=true | all-gather | bytes 163840 | tf_op jit(solution)/shard_map/all_gather | solution.py:38
  24.0 0.4 fusion.24
  24.4 0.3 convert_reduce_fusion.3
  24.7 0.1 stack_reshape.32
  24.8 1.6 %fusion.23 = (f32[128]{0:T(128)S(1)}, f32[128,2048]{1,0:T(8,128)S(1)}) fusion(bf16[2048,1,128]{2,1,0:T(2,128)(2,1)} %get-tuple-element.13, bf16[16,4,8,128]{3,2,1,0:T(8,128)(2,1)S(1)} %bitcast.99), kind=kOutput, calls=%fused_computation.66 | convolution fusion | flops 67633024 | bytes 1606144 | tf_op jit(solution)/shard_map/dot_general | solution.py:11
  26.4 0.3 convert_reduce_fusion.2
  26.7 0.1 stack_reshape.33
  26.8 1.6 %fusion.22 = (f32[128]{0:T(128)S(1)}, f32[128,2048]{1,0:T(8,128)S(1)}) fusion(bf16[2048,1,128]{2,1,0:T(2,128)(2,1)} %get-tuple-element.12, bf16[16,4,8,128]{3,2,1,0:T(8,128)(2,1)S(1)} %bitcast.100), kind=kOutput, calls=%fused_computation.65 | convolution fusion | flops 67633024 | bytes 1606144 | tf_op jit(solution)/shard_map/dot_general | solution.py:11
  28.4 1.0 %copy-done.1 = f32[128,2048]{1,0:T(8,128)} copy-done((f32[128,2048]{1,0:T(8,128)}, f32[128,2048]{1,0:T(8,128)S(1)}, u32[]{:S(2)}) %copy-start.1) | copy-done | bytes 1048600
  29.5 0.3 convert_reduce_fusion.1
  29.8 0.1 stack_reshape.34
  29.8 1.6 %fusion.21 = (f32[128]{0:T(128)S(1)}, f32[128,2048]{1,0:T(8,128)S(1)}) fusion(bf16[2048,1,128]{2,1,0:T(2,128)(2,1)} %get-tuple-element.14, bf16[16,4,8,128]{3,2,1,0:T(8,128)(2,1)S(1)} %bitcast.101), kind=kOutput, calls=%fused_computation.64 | convolution fusion | flops 67633024 | bytes 1606144 | tf_op jit(solution)/shard_map/dot_general | solution.py:11
  31.5 1.0 %copy-done.3 = f32[128,2048]{1,0:T(8,128)} copy-done((f32[128,2048]{1,0:T(8,128)}, f32[128,2048]{1,0:T(8,128)S(1)}, u32[]{:S(2)}) %copy-start.3) | copy-done | bytes 1048600
  32.5 0.3 convert_reduce_fusion
  32.8 0.1 stack_reshape.35
  32.9 0.1 reshape_reshape.11
  33.0 0.7 reshape.116
  33.6 5.0 %all-to-all-start.2 = ((f32[4,1,128]{2,1,0:T(1,128)}), f32[4,1,128]{2,1,0:T(1,128)S(1)}, u32[]{:S(2)}, u32[]{:S(2)}) async-start(f32[4,1,128]{2,1,0:T(1,128)} %reshape.116), calls=%async_computation.2 | async-start | bytes 4096 | tf_op jit(solution)/shard_map/all_to_all | solution.py:106
  38.6 0.1 stack_reshape.28
  38.7 0.1 stack_reshape.29
  38.8 0.1 stack_reshape.30
  38.9 0.1 stack_reshape.31
  39.0 0.1 fusion.11
  39.2 0.6 select_reduce_fusion
  39.8 0.2 convert_reduce_fusion.4
  40.0 8.1 %fusion.20 = (bf16[2048,1,128]{2,1,0:T(2,128)(2,1)S(1)}, bf16[2048,1,128]{2,1,0:T(2,128)(2,1)S(1)}, bf16[2048,1,128]{2,1,0:T(2,128)(2,1)S(1)}, bf16[2048,1,128]{2,1,0:T(2,128)(2,1)S(1)}) fusion(bf16[2048,4,128]{2,1,0:T(4,128)(2,1)} %param.12), kind=kLoop, calls=%fused_computation.63 | loop fusion | bytes 4194304 | tf_op jit(solution)/shard_map/slice | solution.py:47
  48.2 0.4 convolution_bitcast_fusion.3
  48.5 0.4 convolution_bitcast_fusion.2
  48.9 0.5 copy-done.2
  49.4 0.4 convolution_bitcast_fusion.1
  49.7 0.4 convolution_bitcast_fusion
  50.1 0.1 reshape_reshape.9
  50.2 0.7 reshape.114
  50.9 5.1 %all-to-all-start = ((f32[4,1,128]{2,1,0:T(1,128)}), f32[4,1,128]{2,1,0:T(1,128)S(1)}, u32[]{:S(2)}, u32[]{:S(2)}) async-start(f32[4,1,128]{2,1,0:T(1,128)} %reshape.114), calls=%async_computation | async-start | bytes 4096 | tf_op jit(solution)/shard_map/all_to_all | solution.py:103
  56.0 0.1 reshape.101
  56.1 0.1 reshape.107
  56.2 0.7 copy.39
  56.9 0.5 broadcast.26
  57.4 0.7 reduce
  58.1 0.1 reshape.117
  58.2 3.2 %all-to-all-done = f32[4,1,128]{2,1,0:T(1,128)S(1)} async-done(((f32[4,1,128]{2,1,0:T(1,128)}), f32[4,1,128]{2,1,0:T(1,128)S(1)}, u32[]{:S(2)}, u32[]{:S(2)}) %all-to-all-start) | async-done | bytes 2080 | tf_op jit(solution)/shard_map/all_to_all | solution.py:103
  61.4 3.4 %all-to-all-start.1 = ((f32[4,4,32,128]{3,2,1,0:T(8,128)}), f32[4,4,32,128]{3,2,1,0:T(8,128)S(1)}, u32[]{:S(2)}, u32[]{:S(2)}) async-start(f32[4,4,32,128]{3,2,1,0:T(8,128)} %bitcast.30), calls=%async_computation.1 | async-start | bytes 524288 | tf_op jit(solution)/shard_map/all_to_all | solution.py:96
  64.8 0.7 reduce.1
  65.5 0.1 reshape.115
  65.6 5.9 %all-to-all-done.1 = f32[4,4,32,128]{3,2,1,0:T(8,128)S(1)} async-done(((f32[4,4,32,128]{3,2,1,0:T(8,128)}), f32[4,4,32,128]{3,2,1,0:T(8,128)S(1)}, u32[]{:S(2)}, u32[]{:S(2)}) %all-to-all-start.1) | async-done | bytes 262176 | tf_op jit(solution)/shard_map/all_to_all | solution.py:96
  71.6 0.1 multiply_reduce_fusion
  71.7 1.0 %fusion.4 = bf16[4,32,128]{2,1,0:T(8,128)(2,1)} fusion(f32[4,32,128]{2,1,0:T(8,128)S(1)} %multiply_reduce_fusion, bf16[4,192,4,128]{3,2,1,0:T(4,128)(2,1)S(1)} %copy-done.7, f32[4,32]{1,0:T(4,128)S(1)} %get-tuple-element.5, f32[4,32]{1,0:T(4,128)S(1)} %get-tuple-element.6, f32[4,4,128]{2,1,0:T(4,128)S(1)} %convert_element_type.46, ...), kind=kOutput, calls=%fused_computation.14 | convolution fusion | flops 6488064 | bytes 994048 | tf_op jit(solution)/shard_map/bgqs,bsgd->bgqd/dot_general | solution.py:80
  (32 shorter events, 0.3 us)
Async XLA Ops:
  0.0 39.2 %copy-start = (bf16[4,192,4,128]{3,2,1,0:T(4,128)(2,1)S(1)}, bf16[4,192,4,128]{3,2,1,0:T(4,128)(2,1)}, u32[]{:S(2)}) copy-start(bf16[4,192,4,128]{3,2,1,0:T(4,128)(2,1)} %param.13) | copy-start | bytes 2359300
  0.0 8.9 %copy-start.5 = (bf16[4,32,128]{2,1,0:T(8,128)(2,1)S(1)}, bf16[4,32,128]{2,1,0:T(8,128)(2,1)}, u32[]{:S(2)}) copy-start(bf16[4,32,128]{2,1,0:T(8,128)(2,1)} %param.8) | copy-start | bytes 98308
  28.4 1.0 %copy-start.1 = (f32[128,2048]{1,0:T(8,128)}, f32[128,2048]{1,0:T(8,128)S(1)}, u32[]{:S(2)}) copy-start(f32[128,2048]{1,0:T(8,128)S(1)} %get-tuple-element.22) | copy-start | bytes 3145732
  28.4 10.5 %copy-start.8 = (bf16[4,4,128]{2,1,0:T(4,128)(2,1)S(1)}, bf16[4,4,128]{2,1,0:T(4,128)(2,1)}, u32[]{:S(2)}) copy-start(bf16[4,4,128]{2,1,0:T(4,128)(2,1)} %param.9) | copy-start | bytes 12292
  28.4 10.7 %copy-start.9 = (s32[4]{0:T(128)S(1)}, s32[4]{0:T(128)}, u32[]{:S(2)}) copy-start(s32[4]{0:T(128)} %param.15) | copy-start | bytes 52
  31.5 1.0 %copy-start.3 = (f32[128,2048]{1,0:T(8,128)}, f32[128,2048]{1,0:T(8,128)S(1)}, u32[]{:S(2)}) copy-start(f32[128,2048]{1,0:T(8,128)S(1)} %get-tuple-element.20) | copy-start | bytes 3145732
  33.6 17.3 %all-to-all-start.2 = ((f32[4,1,128]{2,1,0:T(1,128)}), f32[4,1,128]{2,1,0:T(1,128)S(1)}, u32[]{:S(2)}, u32[]{:S(2)}) async-start(f32[4,1,128]{2,1,0:T(1,128)} %reshape.116), calls=%async_computation.2 | async-start | bytes 4096 | tf_op jit(solution)/shard_map/all_to_all | solution.py:106
  48.1 1.2 %copy-start.2 = (f32[128,2048]{1,0:T(8,128)S(1)}, f32[128,2048]{1,0:T(8,128)}, u32[]{:S(2)}) copy-start(f32[128,2048]{1,0:T(8,128)} %copy-done.1) | copy-start | bytes 3145732
  48.1 1.6 %copy-start.4 = (f32[128,2048]{1,0:T(8,128)S(1)}, f32[128,2048]{1,0:T(8,128)}, u32[]{:S(2)}) copy-start(f32[128,2048]{1,0:T(8,128)} %copy-done.3) | copy-start | bytes 3145732
  49.4 7.5 %copy-start.6 = (bf16[4,4,128]{2,1,0:T(4,128)(2,1)S(1)}, bf16[4,4,128]{2,1,0:T(4,128)(2,1)}, u32[]{:S(2)}) copy-start(bf16[4,4,128]{2,1,0:T(4,128)(2,1)} %param.10) | copy-start | bytes 12292
  49.7 22.0 %copy-start.7 = (bf16[4,192,4,128]{3,2,1,0:T(4,128)(2,1)S(1)}, bf16[4,192,4,128]{3,2,1,0:T(4,128)(2,1)}, u32[]{:S(2)}) copy-start(bf16[4,192,4,128]{3,2,1,0:T(4,128)(2,1)} %param.14) | copy-start | bytes 2359300
  50.9 10.5 %all-to-all-start = ((f32[4,1,128]{2,1,0:T(1,128)}), f32[4,1,128]{2,1,0:T(1,128)S(1)}, u32[]{:S(2)}, u32[]{:S(2)}) async-start(f32[4,1,128]{2,1,0:T(1,128)} %reshape.114), calls=%async_computation | async-start | bytes 4096 | tf_op jit(solution)/shard_map/all_to_all | solution.py:103
  61.4 10.2 %all-to-all-start.1 = ((f32[4,4,32,128]{3,2,1,0:T(8,128)}), f32[4,4,32,128]{3,2,1,0:T(8,128)S(1)}, u32[]{:S(2)}, u32[]{:S(2)}) async-start(f32[4,4,32,128]{3,2,1,0:T(8,128)} %bitcast.30), calls=%async_computation.1 | async-start | bytes 524288 | tf_op jit(solution)/shard_map/all_to_all | solution.py:96
where the time goes:
time: 73.2 us; the launch traced here: 72.7 us
  local copies, waits for them, and re-layouts  23.3 us (32%)
  blocking collectives  15.1 us (21%)
  starting transfers between devices  13.5 us (18%)
  waiting for transfers between devices  9.17 us (13%)
  matrix products  8.4 us (11%)
  other arithmetic  3.07 us (4%)
    all_gather x1, blocking collectives, body(): gathered = lax.all_gather(queries, 'seq', axis=0, tiled=True)  15.1 us
    slice x1, local copies, waits for them, and re-layouts, body(): shared_prefix_keys[:, kv_head]  8.92 us
    slice x1, local copies, waits for them, and re-layouts, body(): shared_prefix_values[:, kv_head]  8.1 us
    all_to_all x1, waiting for transfers between devices, body(): lax.all_to_all(block_out.reshape(seq_count, own_count, head_count, width)...  5.93 us
    dot_general x4, matrix products, prefix_block(): lax.dot_general(query_rows, block_keys, (((1,), (1,)), ((), ())), preferr...  5.26 us
    all_to_all x1, starting transfers between devices, body(): lax.all_to_all(block_max.reshape(state_shape), 'seq', split_axis=0, conca...  5.09 us
    all_to_all x1, starting transfers between devices, body(): lax.all_to_all(block_total.reshape(state_shape), 'seq', split_axis=0, con...  4.97 us
    unnamed x24, local copies, waits for them, and re-layouts  4.02 us
  transfers between devices with their start and end apart: 3, of which 2 were waited for; matrix products, arithmetic and copies ran while one was open for 20% of the time, Pallas kernels for 0%

commit v1 on v0

v1 whole, which is shorter than its diff:
```python
import functools
import math

import jax
import jax.numpy as jnp
from jax import lax
from jax.experimental import pallas as pl
from jax.experimental.pallas import tpu as pltpu
from jax.sharding import PartitionSpec as P

MESH = pl.DeviceIdType.MESH
BF16 = jnp.bfloat16
F32 = jnp.float32
CHUNKS = 4
LOOP_ROWS = 512


def kernel(
    n,
    kv,
    lengths_ref,
    q_ref,
    fk_ref,
    fv_ref,
    pk_hbm,
    pv_hbm,
    sk_hbm,
    sv_hbm,
    o_ref,
    kraw,
    vraw,
    wide,
    kh,
    vh,
    sk,
    sv,
    qown,
    qall,
    obuf,
    rbuf,
    lo_s,
    lm_s,
    ll_s,
    pre_sem,
    suf_sem,
    qsend,
    qrecv,
    osend,
    orecv,
):
    own, heads, width = q_ref.shape
    group = heads // kv
    rows = own * group
    total_rows = pk_hbm.shape[0]
    positions = total_rows // kv
    chunk = total_rows // CHUNKS
    slots = sk_hbm.shape[1] // kv
    scale = math.log2(math.e) / math.sqrt(width)
    me = lax.axis_index("seq")
    peers = [lax.rem(me + d, n) for d in range(1, n)]

    barrier = pltpu.get_barrier_semaphore()
    for peer in peers:
        pl.semaphore_signal(barrier, inc=1, device_id={"seq": peer}, device_id_type=MESH)

    def prefix_copy(which, c):
        src, dst = ((pk_hbm, kraw), (pv_hbm, vraw))[which]
        span = pl.ds(c * chunk, chunk)
        return pltpu.make_async_copy(src.at[span], dst.at[span], pre_sem.at[which, c])

    suffix_copies = [
        pltpu.make_async_copy(sk_hbm, sk, suf_sem.at[0]),
        pltpu.make_async_copy(sv_hbm, sv, suf_sem.at[1]),
    ]
    for c in range(CHUNKS):
        prefix_copy(0, c).start()
    for copy in suffix_copies:
        copy.start()
    for c in range(CHUNKS):
        prefix_copy(1, c).start()

    q32 = [q_ref[b].astype(F32) for b in range(own)]
    for g in range(kv):
        part = jnp.concatenate([q32[b][g * group : (g + 1) * group] for b in range(own)], axis=0)
        part = part.astype(BF16)
        qown[g] = part
        qall[g, me] = part

    pl.semaphore_wait(barrier, n - 1)

    def query_copy(g, peer):
        return pltpu.make_async_remote_copy(
            src_ref=qown.at[g],
            dst_ref=qall.at[g, me],
            send_sem=qsend.at[g, peer],
            recv_sem=qrecv.at[g, me],
            device_id={"seq": peer},
            device_id_type=MESH,
        )

    def query_arrival(g, peer):
        return pltpu.make_async_remote_copy(
            src_ref=qown.at[g],
            dst_ref=qall.at[g, peer],
            send_sem=qsend.at[g, peer],
            recv_sem=qrecv.at[g, peer],
            device_id={"seq": peer},
            device_id_type=MESH,
        )

    for g in range(kv):
        for peer in peers:
            query_copy(g, peer).start()

    def split_heads(raw, out, c):
        per = LOOP_ROWS // kv

        @pl.loop(0, chunk // LOOP_ROWS)
        def _(i):
            base = pl.multiple_of(c * chunk + i * LOOP_ROWS, LOOP_ROWS)
            wide[...] = raw[pl.ds(base, LOOP_ROWS), :].astype(F32)
            first = pl.multiple_of((c * chunk) // kv + i * per, per)
            for g in range(kv):
                out[g, pl.ds(first, per), :] = wide[pl.ds(g, per, stride=kv), :].astype(BF16)

    for c in range(CHUNKS):
        prefix_copy(0, c).wait()
        split_heads(kraw, kh, c)

    for copy in suffix_copies:
        copy.wait()
    columns = slots * kv
    col = lax.broadcasted_iota(jnp.int32, (heads, columns), 1)
    row = lax.broadcasted_iota(jnp.int32, (heads, columns), 0)
    same_head = lax.rem(col, kv) == row // group
    slot = col // kv
    for b in range(own):
        live = jnp.logical_and(same_head, slot < lengths_ref[b])
        fk = fk_ref[b].astype(F32)
        fv = fv_ref[b].astype(F32)
        fk_rows = jnp.concatenate(
            [jnp.broadcast_to(fk[g : g + 1], (group, width)) for g in range(kv)], axis=0
        )
        fv_rows = jnp.concatenate(
            [jnp.broadcast_to(fv[g : g + 1], (group, width)) for g in range(kv)], axis=0
        )
        own_score = jnp.sum(q32[b] * fk_rows, axis=1, keepdims=True) * scale
        s = (
            lax.dot_general(
                q_ref[b], sk[b], (((1,), (1,)), ((), ())), preferred_element_type=F32
            )
            * scale
        )
        s = jnp.where(live, s, own_score)
        top = jnp.maximum(jnp.max(s, axis=1, keepdims=True), own_score)
        p = jnp.where(live, jnp.exp2(s - top), 0.0).astype(BF16)
        w = jnp.exp2(own_score - top).astype(BF16).astype(F32)
        total = jnp.sum(p.astype(F32), axis=1, keepdims=True) + w
        out = jnp.dot(p, sv[b], preferred_element_type=F32) + w * fv_rows
        top = jnp.broadcast_to(top, (heads, width))
        total = jnp.broadcast_to(total, (heads, width))
        for g in range(kv):
            dst = pl.ds(b * group, group)
            src = slice(g * group, (g + 1) * group)
            lo_s[g, dst, :] = out[src]
            lm_s[g, dst, :] = top[src]
            ll_s[g, dst, :] = total[src]

    for c in range(CHUNKS):
        prefix_copy(1, c).wait()
        split_heads(vraw, vh, c)

    lane = lax.broadcasted_iota(jnp.int32, (rows, width), 1)
    line = lax.broadcasted_iota(jnp.int32, (rows, width), 0)
    is_max = lane == line
    is_total = lane == line + rows

    def out_copy(g, peer):
        return pltpu.make_async_remote_copy(
            src_ref=obuf.at[g, peer],
            dst_ref=rbuf.at[g, me],
            send_sem=osend.at[g, peer],
            recv_sem=orecv.at[g, me],
            device_id={"seq": peer},
            device_id_type=MESH,
        )

    def out_arrival(g, peer):
        return pltpu.make_async_remote_copy(
            src_ref=obuf.at[g, peer],
            dst_ref=rbuf.at[g, peer],
            send_sem=osend.at[g, peer],
            recv_sem=orecv.at[g, peer],
            device_id={"seq": peer},
            device_id_type=MESH,
        )

    def scores(g):
        for peer in peers:
            query_arrival(g, peer).wait_recv()
        return lax.dot_general(
            qall[g].reshape(n * rows, width),
            kh[g],
            (((1,), (1,)), ((), ())),
            preferred_element_type=F32,
        )

    for g in range(kv):
        s = scores(g) * scale
        top = jnp.max(s, axis=1, keepdims=True)
        p = jnp.exp2(s - top).astype(BF16)
        total = jnp.sum(p.astype(F32), axis=1, keepdims=True)
        out = jnp.dot(p, vh[g], preferred_element_type=F32)
        for j in range(n):
            block = slice(j * rows, (j + 1) * rows)
            obuf[g, j, 0:rows, :] = out[block]
            stats = jnp.where(is_max, top[block], jnp.where(is_total, total[block], 0.0))
            obuf[g, j, rows : rows + 1, :] = jnp.sum(stats, axis=0, keepdims=True)
        for peer in peers:
            out_copy(g, peer).start()

    def columns_of(stat):
        wide_stat = jnp.broadcast_to(stat, (rows, width))
        m = jnp.sum(jnp.where(is_max, wide_stat, 0.0), axis=1, keepdims=True)
        t = jnp.sum(jnp.where(is_total, wide_stat, 0.0), axis=1, keepdims=True)
        return m, t

    for g in range(kv):
        for peer in peers:
            out_arrival(g, peer).wait_recv()
        parts = [(obuf, me)] + [(rbuf, peer) for peer in peers]
        stats = [columns_of(buf[g, j, rows : rows + 1, :]) for buf, j in parts]
        lm = lm_s[g]
        highest = lm
        for m, _ in stats:
            highest = jnp.maximum(highest, m)
        local_scale = jnp.exp2(lm - highest)
        total = ll_s[g] * local_scale
        numerator = lo_s[g] * local_scale
        for (buf, j), (m, t) in zip(parts, stats):
            factor = jnp.exp2(m - highest)
            total = total + t * factor
            numerator = numerator + buf[g, j, 0:rows, :] * factor
        context = (numerator / total).astype(BF16)
        for b in range(own):
            o_ref[b, g * group : (g + 1) * group, :] = context[b * group : (b + 1) * group]

    for g in range(kv):
        for peer in peers:
            query_copy(g, peer).wait_send()
            out_copy(g, peer).wait_send()


def body(
    n,
    queries,
    fresh_token_keys,
    fresh_token_values,
    shared_prefix_keys,
    shared_prefix_values,
    sequence_suffix_keys,
    sequence_suffix_values,
    suffix_lengths,
):
    own, heads, width = queries.shape
    positions, kv, _ = shared_prefix_keys.shape
    slots = sequence_suffix_keys.shape[1]
    rows = own * (heads // kv)
    total_rows = positions * kv
    any_spec = pl.BlockSpec(memory_space=pl.ANY)
    vmem_spec = pl.BlockSpec(memory_space=pltpu.VMEM)
    return pl.pallas_call(
        functools.partial(kernel, n, kv),
        out_shape=jax.ShapeDtypeStruct(queries.shape, BF16),
        in_specs=[pl.BlockSpec(memory_space=pltpu.SMEM)] + [vmem_spec] * 3 + [any_spec] * 4,
        out_specs=vmem_spec,
        scratch_shapes=[
            pltpu.VMEM((total_rows, width), BF16),
            pltpu.VMEM((total_rows, width), BF16),
            pltpu.VMEM((LOOP_ROWS, width), F32),
            pltpu.VMEM((kv, positions, width), BF16),
            pltpu.VMEM((kv, positions, width), BF16),
            pltpu.VMEM((own, slots * kv, width), BF16),
            pltpu.VMEM((own, slots * kv, width), BF16),
            pltpu.VMEM((kv, rows, width), BF16),
            pltpu.VMEM((kv, n, rows, width), BF16),
            pltpu.VMEM((kv, n, rows + 1, width), F32),
            pltpu.VMEM((kv, n, rows + 1, width), F32),
            pltpu.VMEM((kv, rows, width), F32),
            pltpu.VMEM((kv, rows, width), F32),
            pltpu.VMEM((kv, rows, width), F32),
            pltpu.SemaphoreType.DMA((2, CHUNKS)),
            pltpu.SemaphoreType.DMA((2,)),
            pltpu.SemaphoreType.DMA((kv, n)),
            pltpu.SemaphoreType.DMA((kv, n)),
            pltpu.SemaphoreType.DMA((kv, n)),
            pltpu.SemaphoreType.DMA((kv, n)),
        ],
        compiler_params=pltpu.CompilerParams(
            collective_id=0, has_side_effects=True, vmem_limit_bytes=60 * 1024 * 1024
        ),
        name="decode_attention",
    )(
        suffix_lengths,
        queries,
        fresh_token_keys,
        fresh_token_values,
        shared_prefix_keys.reshape(total_rows, width),
        shared_prefix_values.reshape(total_rows, width),
        sequence_suffix_keys.reshape(own, slots * kv, width),
        sequence_suffix_values.reshape(own, slots * kv, width),
    )


def solution(mesh):
    in_specs = (
        P(("groups", "seq", "batch"), "head", None),
        P(("groups", "seq", "batch"), "head", None),
        P(("groups", "seq", "batch"), "head", None),
        P(("groups", "seq"), "head", None),
        P(("groups", "seq"), "head", None),
        P(("groups", "seq", "batch"), None, "head", None),
        P(("groups", "seq", "batch"), None, "head", None),
        P(("groups", "seq", "batch")),
    )
    out_specs = P(("groups", "seq", "batch"), "head", None)
    return jax.shard_map(
        functools.partial(body, mesh.shape["seq"]),
        mesh=mesh,
        in_specs=in_specs,
        out_specs=out_specs,
        check_vma=False,
    )
```

time: 73.2 us -> 20 us (0.27)
  local copies, waits for them, and re-layouts: 23.3 us -> 1.38 us
  Pallas kernels: 0 us -> 18.3 us
  blocking collectives: 15.1 us -> 0 us
  starting transfers between devices: 13.5 us -> 0 us
  waiting for transfers between devices: 9.17 us -> 0 us
  matrix products: 8.4 us -> 0 us
  other arithmetic: 3.07 us -> 0 us
    pallas_call x0 -> x1, Pallas kernels: none -> 18.3 us  [body(): pl.pallas_call(functools.partial(kernel, n, kv), out_shape=jax.ShapeDtype...]
    slice x2 -> x0, local copies, waits for them, and re-layouts: 17 us -> none  [the longest x1 8.92 us: body(): shared_prefix_keys[:, kv_head]]
    all_gather x1 -> x0, blocking collectives: 15.1 us -> none  [body(): gathered = lax.all_gather(queries, 'seq', axis=0, tiled=True)]
    all_to_all x3 -> x0, starting transfers between devices: 13.5 us -> none  [the longest x1 5.09 us: body(): lax.all_to_all(block_max.reshape(state_shape), 'seq', split_axis=0, conca...]
    all_to_all x3 -> x0, waiting for transfers between devices: 9.17 us -> none  [the longest x1 5.93 us: body(): lax.all_to_all(block_out.reshape(seq_count, own_count, head_count, width)...]
    dot_general x11 -> x0, matrix products: 8.4 us -> none  [the longest x4 5.26 us: prefix_block(): lax.dot_general(query_rows, block_keys, (((1,), (1,)), ((), ())), preferr...]
    unnamed x24 -> x1, local copies, waits for them, and re-layouts: 4.02 us -> 1.38 us
    another operation x13 -> x0, local copies, waits for them, and re-layouts: 1.6 us -> none  [the longest x1 0.72 us: body(): jnp.stack(outputs_list, axis=1).reshape(row_count, head_count, width)]
  transfers between devices with their start and end apart: 3 -> 0, of which waited for: 2 -> 0; matrix products, arithmetic and copies ran while one was open for 20% -> 0% of each run, Pallas kernels for 0% -> 0%
where the time goes in v1:
time: 20 us; the launch traced here: 19.7 us
  Pallas kernels  18.3 us (92%)
  local copies, waits for them, and re-layouts  1.38 us (7%)
    pallas_call x1, Pallas kernels, body(): pl.pallas_call(functools.partial(kernel, n, kv), out_shape=jax.ShapeDtype...  18.3 us
    unnamed x1, local copies, waits for them, and re-layouts  1.38 us

profile of v1, /device:TPU:0, one launch (start us, length us, event | category | flops | bytes accessed | tf_op | source)
XLA Modules:
  0.0 19.7 jit_solution(13378392349396841000)
XLA Ops:
  0.0 18.3 %decode_attention.1 = bf16[4,32,128]{2,1,0:T(8,128)(2,1)} custom-call(s32[4]{0:T(128)} %lengths_ref.1, bf16[4,32,128]{2,1,0:T(8,128)(2,1)} %q_ref.1, bf16[4,4,128]{2,1,0:T(4,128)(2,1)} %fk_ref.1, bf16[4,4,128]{2,1,0:T(4,128)(2,1)} %fv_ref.1, bf16[8192,128]{1,0:T(8,128)(2,1)} %bitcast.4, bf16[8192,128]{1,0:T(8,128)(2,1)} %bitcast.5, ...), custom_call_target="tpu_custom_call" | custom-call | tf_op jit(solution)/shard_map/decode_attention/pallas_call | solution.py:272
  18.3 1.4 %copy.10 = bf16[4,32,128]{2,1,0:T(8,128)(2,1)} copy(bf16[4,32,128]{2,1,0:T(8,128)(2,1)} %decode_attention.1) | data formatting | bytes 65536

commit v2 on v1

--- a/solution.py
+++ b/solution.py
@@ -13,20 +13,27 @@
 F32 = jnp.float32
 CHUNKS = 4
 LOOP_ROWS = 512
+CODE_MAX = 32767.0
+QUERY_HEADS = 2
+VMEM_BYTES = 60 * 1024 * 1024
 
 
 def kernel(
     n,
     kv,
-    lengths_ref,
-    q_ref,
-    fk_ref,
-    fv_ref,
+    lengths_hbm,
+    q_hbm,
+    fk_hbm,
+    fv_hbm,
     pk_hbm,
     pv_hbm,
     sk_hbm,
     sv_hbm,
     o_ref,
+    lengths_ref,
+    q_ref,
+    fk_ref,
+    fv_ref,
     kraw,
     vraw,
     wide,
@@ -38,19 +45,25 @@
     qall,
     obuf,
     rbuf,
+    ostat,
+    rstat,
     lo_s,
     lm_s,
     ll_s,
+    small_sem,
     pre_sem,
     suf_sem,
     qsend,
     qrecv,
     osend,
     orecv,
+    ssend,
+    srecv,
 ):
-    own, heads, width = q_ref.shape
+    own, heads, width = q_hbm.shape
     group = heads // kv
     rows = own * group
+    half = rows // 2
     total_rows = pk_hbm.shape[0]
     positions = total_rows // kv
     chunk = total_rows // CHUNKS
@@ -62,6 +75,15 @@
     barrier = pltpu.get_barrier_semaphore()
     for peer in peers:
         pl.semaphore_signal(barrier, inc=1, device_id={"seq": peer}, device_id_type=MESH)
+
+    small_copies = [
+        pltpu.make_async_copy(src, dst, small_sem.at[i])
+        for i, (src, dst) in enumerate(
+            ((q_hbm, q_ref), (fk_hbm, fk_ref), (fv_hbm, fv_ref), (lengths_hbm, lengths_ref))
+        )
+    ]
+    for copy in small_copies:
+        copy.start()
 
     def prefix_copy(which, c):
         src, dst = ((pk_hbm, kraw), (pv_hbm, vraw))[which]
@@ -79,38 +101,30 @@
     for c in range(CHUNKS):
         prefix_copy(1, c).start()
 
+    small_copies[0].wait()
     q32 = [q_ref[b].astype(F32) for b in range(own)]
     for g in range(kv):
         part = jnp.concatenate([q32[b][g * group : (g + 1) * group] for b in range(own)], axis=0)
         part = part.astype(BF16)
         qown[g] = part
-        qall[g, me] = part
 
     pl.semaphore_wait(barrier, n - 1)
 
-    def query_copy(g, peer):
+    def query_copy(h, d, slot):
+        span = pl.ds(h * QUERY_HEADS, QUERY_HEADS)
         return pltpu.make_async_remote_copy(
-            src_ref=qown.at[g],
-            dst_ref=qall.at[g, me],
-            send_sem=qsend.at[g, peer],
-            recv_sem=qrecv.at[g, me],
-            device_id={"seq": peer},
+            src_ref=qown.at[span],
+            dst_ref=qall.at[slot, span],
+            send_sem=qsend.at[h, d - 1],
+            recv_sem=qrecv.at[h, slot],
+            device_id={"seq": peers[d - 1]},
             device_id_type=MESH,
         )
 
-    def query_arrival(g, peer):
-        return pltpu.make_async_remote_copy(
-            src_ref=qown.at[g],
-            dst_ref=qall.at[g, peer],
-            send_sem=qsend.at[g, peer],
-            recv_sem=qrecv.at[g, peer],
-            device_id={"seq": peer},
-            device_id_type=MESH,
-        )
-
-    for g in range(kv):
-        for peer in peers:
-            query_copy(g, peer).start()
+    query_parts = kv // QUERY_HEADS
+    for h in range(query_parts):
+        for d in range(1, n):
+            query_copy(h, d, n - d - 1).start()
 
     def split_heads(raw, out, c):
         per = LOOP_ROWS // kv
@@ -127,7 +141,7 @@
         prefix_copy(0, c).wait()
         split_heads(kraw, kh, c)
 
-    for copy in suffix_copies:
+    for copy in suffix_copies + small_copies[1:]:
         copy.wait()
     columns = slots * kv
     col = lax.broadcasted_iota(jnp.int32, (heads, columns), 1)
@@ -174,81 +188,111 @@
     line = lax.broadcasted_iota(jnp.int32, (rows, width), 0)
     is_max = lane == line
     is_total = lane == line + rows
-
-    def out_copy(g, peer):
-        return pltpu.make_async_remote_copy(
-            src_ref=obuf.at[g, peer],
-            dst_ref=rbuf.at[g, me],
-            send_sem=osend.at[g, peer],
-            recv_sem=orecv.at[g, me],
-            device_id={"seq": peer},
-            device_id_type=MESH,
-        )
-
-    def out_arrival(g, peer):
-        return pltpu.make_async_remote_copy(
-            src_ref=obuf.at[g, peer],
-            dst_ref=rbuf.at[g, peer],
-            send_sem=osend.at[g, peer],
-            recv_sem=orecv.at[g, peer],
-            device_id={"seq": peer},
-            device_id_type=MESH,
-        )
-
-    def scores(g):
-        for peer in peers:
-            query_arrival(g, peer).wait_recv()
-        return lax.dot_general(
-            qall[g].reshape(n * rows, width),
-            kh[g],
-            (((1,), (1,)), ((), ())),
-            preferred_element_type=F32,
-        )
-
-    for g in range(kv):
-        s = scores(g) * scale
+    is_size = lane == line + 2 * rows
+
+    def returns(g, d, slot):
+        return [
+            pltpu.make_async_remote_copy(
+                src_ref=src.at[g, d - 1],
+                dst_ref=dst.at[g, slot],
+                send_sem=send.at[g, d - 1],
+                recv_sem=recv.at[g, slot],
+                device_id={"seq": peers[d - 1]},
+                device_id_type=MESH,
+            )
+            for src, dst, send, recv in (
+                (ostat, rstat, ssend, srecv),
+                (obuf, rbuf, osend, orecv),
+            )
+        ]
+
+    def attend(s, g):
+        s = s * scale
         top = jnp.max(s, axis=1, keepdims=True)
         p = jnp.exp2(s - top).astype(BF16)
         total = jnp.sum(p.astype(F32), axis=1, keepdims=True)
-        out = jnp.dot(p, vh[g], preferred_element_type=F32)
-        for j in range(n):
-            block = slice(j * rows, (j + 1) * rows)
-            obuf[g, j, 0:rows, :] = out[block]
+        return top, total, jnp.dot(p, vh[g], preferred_element_type=F32)
+
+    def scores(g, query_rows):
+        return lax.dot_general(
+            query_rows, kh[g], (((1,), (1,)), ((), ())), preferred_element_type=F32
+        )
+
+    def remote_scores(g):
+        if g % QUERY_HEADS == 0:
+            for d in range(1, n):
+                query_copy(g // QUERY_HEADS, d, d - 1).wait_recv()
+        return scores(g, jnp.concatenate([qall[d - 1, g] for d in range(1, n)], axis=0))
+
+    own_next = scores(0, qown[0])
+    for g in range(kv):
+        s = own_next
+        if g + 1 < kv:
+            own_next = scores(g + 1, qown[g + 1])
+        top, total, out = attend(s, g)
+        lm = lm_s[g]
+        highest = jnp.maximum(lm, top)
+        local_scale = jnp.exp2(lm - highest)
+        block_scale = jnp.exp2(top - highest)
+        lm_s[g] = highest
+        ll_s[g] = ll_s[g] * local_scale + total * block_scale
+        lo_s[g] = lo_s[g] * local_scale + out * block_scale
+
+    following = remote_scores(0)
+    for g in range(kv):
+        s = following
+        if g + 1 < kv:
+            following = remote_scores(g + 1)
+        top, total, out = attend(s, g)
+        size = jnp.maximum(jnp.max(jnp.abs(out), axis=1, keepdims=True), 1e-30)
+        coded = jnp.floor(out * (CODE_MAX / size) + 0.5).astype(jnp.int32)
+        for d in range(1, n):
+            block = slice((d - 1) * rows, d * rows)
             stats = jnp.where(is_max, top[block], jnp.where(is_total, total[block], 0.0))
-            obuf[g, j, rows : rows + 1, :] = jnp.sum(stats, axis=0, keepdims=True)
-        for peer in peers:
-            out_copy(g, peer).start()
+            stats = jnp.where(is_size, size[block], stats)
+            ostat[g, d - 1] = jnp.sum(stats, axis=0, keepdims=True)
+            high = coded[(d - 1) * rows : (d - 1) * rows + half]
+            low = coded[(d - 1) * rows + half : d * rows]
+            obuf[g, d - 1] = (high << 16) | (low & 0xFFFF)
+        for d in range(1, n):
+            for copy in returns(g, d, n - d - 1):
+                copy.start()
 
     def columns_of(stat):
         wide_stat = jnp.broadcast_to(stat, (rows, width))
-        m = jnp.sum(jnp.where(is_max, wide_stat, 0.0), axis=1, keepdims=True)
-        t = jnp.sum(jnp.where(is_total, wide_stat, 0.0), axis=1, keepdims=True)
-        return m, t
+        return [
+            jnp.sum(jnp.where(mask, wide_stat, 0.0), axis=1, keepdims=True)
+            for mask in (is_max, is_total, is_size)
+        ]
 
     for g in range(kv):
-        for peer in peers:
-            out_arrival(g, peer).wait_recv()
-        parts = [(obuf, me)] + [(rbuf, peer) for peer in peers]
-        stats = [columns_of(buf[g, j, rows : rows + 1, :]) for buf, j in parts]
+        for d in range(1, n):
+            for copy in returns(g, d, d - 1):
+                copy.wait_recv()
+        stats = [columns_of(rstat[g, d - 1]) for d in range(1, n)]
         lm = lm_s[g]
         highest = lm
-        for m, _ in stats:
+        for m, _, _ in stats:
             highest = jnp.maximum(highest, m)
         local_scale = jnp.exp2(lm - highest)
         total = ll_s[g] * local_scale
         numerator = lo_s[g] * local_scale
-        for (buf, j), (m, t) in zip(parts, stats):
+        for d, (m, t, a) in enumerate(stats, 1):
             factor = jnp.exp2(m - highest)
             total = total + t * factor
-            numerator = numerator + buf[g, j, 0:rows, :] * factor
+            words = rbuf[g, d - 1]
+            codes = jnp.concatenate([words >> 16, (words << 16) >> 16], axis=0)
+            numerator = numerator + codes.astype(F32) * (a * (factor * (1.0 / CODE_MAX)))
         context = (numerator / total).astype(BF16)
         for b in range(own):
             o_ref[b, g * group : (g + 1) * group, :] = context[b * group : (b + 1) * group]
 
-    for g in range(kv):
-        for peer in peers:
-            query_copy(g, peer).wait_send()
-            out_copy(g, peer).wait_send()
+    for d in range(1, n):
+        for h in range(query_parts):
+            query_copy(h, d, n - d - 1).wait_send()
+        for g in range(kv):
+            for copy in returns(g, d, n - d - 1):
+                copy.wait_send()
 
 
 def body(
@@ -267,14 +311,18 @@
     slots = sequence_suffix_keys.shape[1]
     rows = own * (heads // kv)
     total_rows = positions * kv
-    any_spec = pl.BlockSpec(memory_space=pl.ANY)
+    hbm_spec = pl.BlockSpec(memory_space=pltpu.HBM)
     vmem_spec = pl.BlockSpec(memory_space=pltpu.VMEM)
     return pl.pallas_call(
         functools.partial(kernel, n, kv),
         out_shape=jax.ShapeDtypeStruct(queries.shape, BF16),
-        in_specs=[pl.BlockSpec(memory_space=pltpu.SMEM)] + [vmem_spec] * 3 + [any_spec] * 4,
+        in_specs=[hbm_spec] * 8,
         out_specs=vmem_spec,
         scratch_shapes=[
+            pltpu.SMEM(suffix_lengths.shape, jnp.int32),
+            pltpu.VMEM(queries.shape, BF16),
+            pltpu.VMEM(fresh_token_keys.shape, BF16),
+            pltpu.VMEM(fresh_token_values.shape, BF16),
             pltpu.VMEM((total_rows, width), BF16),
             pltpu.VMEM((total_rows, width), BF16),
             pltpu.VMEM((LOOP_ROWS, width), F32),
@@ -283,21 +331,26 @@
             pltpu.VMEM((own, slots * kv, width), BF16),
             pltpu.VMEM((own, slots * kv, width), BF16),
             pltpu.VMEM((kv, rows, width), BF16),
-            pltpu.VMEM((kv, n, rows, width), BF16),
-            pltpu.VMEM((kv, n, rows + 1, width), F32),
-            pltpu.VMEM((kv, n, rows + 1, width), F32),
+            pltpu.VMEM((n - 1, kv, rows, width), BF16),
+            pltpu.VMEM((kv, n - 1, rows // 2, width), jnp.int32),
+            pltpu.VMEM((kv, n - 1, rows // 2, width), jnp.int32),
+            pltpu.VMEM((kv, n - 1, 1, width), F32),
+            pltpu.VMEM((kv, n - 1, 1, width), F32),
             pltpu.VMEM((kv, rows, width), F32),
             pltpu.VMEM((kv, rows, width), F32),
             pltpu.VMEM((kv, rows, width), F32),
+            pltpu.SemaphoreType.DMA((4,)),
             pltpu.SemaphoreType.DMA((2, CHUNKS)),
             pltpu.SemaphoreType.DMA((2,)),
-            pltpu.SemaphoreType.DMA((kv, n)),
-            pltpu.SemaphoreType.DMA((kv, n)),
-            pltpu.SemaphoreType.DMA((kv, n)),
-            pltpu.SemaphoreType.DMA((kv, n)),
+            pltpu.SemaphoreType.DMA((kv, n - 1)),
+            pltpu.SemaphoreType.DMA((kv, n - 1)),
+            pltpu.SemaphoreType.DMA((kv, n - 1)),
+            pltpu.SemaphoreType.DMA((kv, n - 1)),
+            pltpu.SemaphoreType.DMA((kv, n - 1)),
+            pltpu.SemaphoreType.DMA((kv, n - 1)),
         ],
         compiler_params=pltpu.CompilerParams(
-            collective_id=0, has_side_effects=True, vmem_limit_bytes=60 * 1024 * 1024
+            collective_id=0, has_side_effects=True, vmem_limit_bytes=VMEM_BYTES
         ),
         name="decode_attention",
     )(

time: 20 us -> 18 us (0.900)
  Pallas kernels: 18.3 us -> 16.5 us
    pallas_call x1, Pallas kernels: 18.3 us -> 16.5 us  [body(): pl.pallas_call(functools.partial(kernel, n, kv), out_shape=jax.ShapeDtype...]
where the time goes in v2:
time: 18 us; the launch traced here: 17.8 us
  Pallas kernels  16.5 us (92%)
  local copies, waits for them, and re-layouts  1.38 us (8%)
    pallas_call x1, Pallas kernels, body(): pl.pallas_call(functools.partial(kernel, n, kv), out_shape=jax.ShapeDtype...  16.5 us
    unnamed x1, local copies, waits for them, and re-layouts  1.38 us

profile of v2, /device:TPU:0, one launch (start us, length us, event | category | flops | bytes accessed | tf_op | source)
XLA Modules:
  0.0 17.8 jit_solution(899786658690630552)
XLA Ops:
  0.0 16.5 %decode_attention.1 = bf16[4,32,128]{2,1,0:T(8,128)(2,1)} custom-call(s32[4]{0:T(128)} %lengths_hbm.1, bf16[4,32,128]{2,1,0:T(8,128)(2,1)} %q_hbm.1, bf16[4,4,128]{2,1,0:T(4,128)(2,1)} %fk_hbm.1, bf16[4,4,128]{2,1,0:T(4,128)(2,1)} %fv_hbm.1, bf16[8192,128]{1,0:T(8,128)(2,1)} %bitcast.4, bf16[8192,128]{1,0:T(8,128)(2,1)} %bitcast.5, ...), custom_call_target="tpu_custom_call" | custom-call | tf_op jit(solution)/shard_map/decode_attention/pallas_call | solution.py:316
  16.5 1.4 %copy.10 = bf16[4,32,128]{2,1,0:T(8,128)(2,1)} copy(bf16[4,32,128]{2,1,0:T(8,128)(2,1)} %decode_attention.1) | data formatting | bytes 65536
